TPU v7x, 32 devices: a whole 2x2x4 slice. The times are simulated.
32 devices in a mesh: blk: 16 (over z, y, x), grp: 2 (over core).
Axes of the slice: x: 2, y: 2, z: 4, core: 2. Of those that a mesh axis runs over, the one named last changes fastest.
Arguments:
- returns: float32 [512, 8192], P(None, ('blk', 'grp')), may hold values from -200 to 200
Outputs:
- correlation: bfloat16 [8192, 8192], P(('blk', 'grp'))
All inputs are finite; a program needn't handle non-finite values.
Results may differ from a plain program's by a relative error of at most 0.0034.
Values may be sent and summed in bfloat16 or wider, within the bound.
A program may use at most 128 MiB of HBM per device.

v0:
```python
import math
import jax
import jax.numpy as jnp
from jax import lax
from jax.sharding import PartitionSpec as P


def gram_tile(first, second):
    return lax.dot_general(
        first, second, (((0,), (0,)), ((), ())), preferred_element_type=jnp.float32
    )


def shards(returns):
    bar_count = returns.shape[0]
    series_dev = returns.shape[1]
    devices = lax.axis_size(("blk", "grp"))
    my_index = lax.axis_index(("blk", "grp"))
    summed = lax.psum(jnp.sum(returns, axis=1), ("blk", "grp"))
    market = summed / (series_dev * devices)
    excess = returns - market[:, None]
    deviation = excess - jnp.mean(excess, axis=0, keepdims=True)
    inverse = lax.rsqrt(jnp.mean(deviation * deviation, axis=0, keepdims=True) + 1e-06) / math.sqrt(
        bar_count
    )
    zscores = (deviation * inverse).astype(jnp.bfloat16)
    piece = lax.all_gather(zscores, ("blk", "grp"), axis=1, tiled=True)
    products = gram_tile(zscores, piece)
    column_block = jnp.arange(piece.shape[1], dtype=jnp.int32) // series_dev
    return jnp.where(column_block[None, :] >= my_index, products, jnp.float32(0.0)).astype(
        jnp.bfloat16
    )


def solution(mesh):
    in_specs = (P(None, ("blk", "grp")),)
    out_specs = P(("blk", "grp"), None)
    return jax.shard_map(shards, mesh=mesh, in_specs=in_specs, out_specs=out_specs, check_vma=False)
```

profile of v0, /device:TPU:0, one launch (start us, length us, event | category | flops | bytes accessed | tf_op | source)
XLA Modules:
  0.0 158.5 jit_solution(11532635164527842564)
XLA Ops:
  6.5 0.0 all-gather.2.cloned.1.call-start
  6.5 1.2 reduce_sum.27
  7.7 42.0 %psum.7 = f32[512]{0:T(512)S(1)} all-reduce(f32[512]{0:T(512)S(1)} %reduce_sum.27), channel_id=1, replica_groups=mesh['blk'=16,'grp'=2] {'blk','grp'}, use_global_device_ids=true, to_apply=%region_1.0 | all-reduce | flops 512 | bytes 4096 | tf_op jit(solution)/shard_map/psum | solution.py:19
  49.7 1.2 subtract_reduce_fusion
  50.9 1.2 multiply_reduce_fusion
  52.1 1.9 %multiply_convert_fusion = bf16[512,256]{1,0:T(8,128)(2,1)} fusion(f32[512,256]{1,0:T(8,128)} %param.1, f32[256]{0:T(256)S(1)} %rsqrt_multiply_fusion, f32[256]{0:T(256)S(1)} %broadcast_multiply_fusion.1, f32[512]{0:T(512)S(1)} %broadcast_multiply_fusion), kind=kLoop, calls=%fused_computation.2 | loop fusion | flops 524288 | bytes 790528 | tf_op jit(solution)/shard_map/convert_element_type | solution.py:26
  54.0 0.0 all-gather.2.cloned.1.call-update
  54.1 89.7 %all-gather.2.cloned.1.call-done = bf16[512,8192]{1,0:T(8,128)(2,1)} async-done(((bf16[512,256]{1,0:T(8,128)(2,1)}), bf16[512,8192]{1,0:T(8,128)(2,1)}) %all-gather.2.cloned.1.call-update) | async-done | bytes 8388624 | tf_op jit(solution)/shard_map/all_gather | solution.py:27
  143.7 7.9 %fusion = bf16[256,8192]{1,0:T(8,128)(2,1)} fusion(bf16[512,256]{1,0:T(8,128)(2,1)} %multiply_convert_fusion, bf16[512,8192]{1,0:T(8,128)(2,1)} %all-gather.2.cloned.1.call-done, pred[8192]{0:T(1024)(128)(4,1)S(1)} %fusion.1), kind=kOutput, calls=%fused_computation.1 | convolution fusion | flops 2151677952 | bytes 12853248 | tf_op jit(solution)/shard_map/dot_general | solution.py:9
  (4 shorter events, 0.0 us)
Async XLA Ops:
  6.5 137.2 %all-gather.2.cloned.1.call-start = ((), (), s32[]{:S(2)}) async-start(), calls=%async_computation | async-start | bytes 8650752 | tf_op jit(solution)/shard_map/all_gather | solution.py:27
Sparse Core Ops, SparseCore 0:
  54.2 89.5 all-gather.1
where the time goes:
time: 159 us; the launch traced here: 158 us
  waiting for transfers between devices  89.7 us (56%)
  blocking collectives  42 us (26%)
  between operations  13.4 us (8%)
  matrix products  7.89 us (5%)
  other arithmetic  5.49 us (3%)
    all_gather x1, waiting for transfers between devices, shards(): piece = lax.all_gather(zscores, ('blk', 'grp'), axis=1, tiled=True)  89.7 us
    psum x1, blocking collectives, shards(): summed = lax.psum(jnp.sum(returns, axis=1), ('blk', 'grp'))  42 us
    dot_general x1, matrix products, gram_tile(): lax.dot_general(first, second, (((0,), (0,)), ((), ())), preferred_elemen...  7.89 us
  transfers between devices with their start and end apart: 1, of which 1 were waited for; matrix products, arithmetic and copies ran while one was open for 0% of the time, Pallas kernels for 0%

commit v1 on v0

--- a/solution.py
+++ b/solution.py
@@ -16,7 +16,7 @@
     series_dev = returns.shape[1]
     devices = lax.axis_size(("blk", "grp"))
     my_index = lax.axis_index(("blk", "grp"))
-    summed = lax.psum(jnp.sum(returns, axis=1), ("blk", "grp"))
+    summed = lax.psum(lax.psum(jnp.sum(returns, axis=1), "grp"), "blk")
     market = summed / (series_dev * devices)
     excess = returns - market[:, None]
     deviation = excess - jnp.mean(excess, axis=0, keepdims=True)

time: 159 us -> 159 us (level)
  blocking collectives: 42 us -> 46 us
  waiting for transfers between devices: 89.7 us -> 85.7 us
    psum x1 -> x2, blocking collectives: 42 us -> 46 us  [shards(): summed = lax.psum(lax.psum(jnp.sum(returns, axis=1), 'grp'), 'blk')]
    all_gather x1, waiting for transfers between devices: 89.7 us -> 85.7 us  [shards(): piece = lax.all_gather(zscores, ('blk', 'grp'), axis=1, tiled=True)]
where the time goes in v1:
time: 159 us
  waiting for transfers between devices  85.7 us (54%)
  blocking collectives  46 us (29%)
  between operations  13.4 us (8%)
  matrix products  7.89 us (5%)
  other arithmetic  5.5 us (3%)
    all_gather x1, waiting for transfers between devices, shards(): piece = lax.all_gather(zscores, ('blk', 'grp'), axis=1, tiled=True)  85.7 us
    psum x2, blocking collectives, shards(): summed = lax.psum(lax.psum(jnp.sum(returns, axis=1), 'grp'), 'blk')  46 us
    dot_general x1, matrix products, gram_tile(): lax.dot_general(first, second, (((0,), (0,)), ((), ())), preferred_elemen...  7.89 us
  transfers between devices with their start and end apart: 1, of which 1 were waited for; matrix products, arithmetic and copies ran while one was open for 0% of the time, Pallas kernels for 0%

profile of v1, /device:TPU:0, one launch (start us, length us, event | category | flops | bytes accessed | tf_op | source)
XLA Modules:
  0.0 158.5 jit_solution(8566085006919442909)
XLA Ops:
  6.5 0.0 all-gather.2.cloned.1.call-start
  6.5 1.2 reduce_sum.27
  7.7 2.6 %psum.14 = f32[512]{0:T(512)S(1)} all-reduce(f32[512]{0:T(512)S(1)} %reduce_sum.27), channel_id=1, replica_groups=mesh['blk'=16,'grp'=2] {'grp'}, use_global_device_ids=true, to_apply=%region_1.0 | all-reduce | flops 512 | bytes 4096 | tf_op jit(solution)/shard_map/psum | solution.py:19
  10.4 43.3 %psum.15 = f32[512]{0:T(512)S(1)} all-reduce(f32[512]{0:T(512)S(1)} %psum.14), channel_id=1, replica_groups=mesh['blk'=16,'grp'=2] {'blk'}, use_global_device_ids=true, to_apply=%region_2.0 | all-reduce | flops 512 | bytes 4096 | tf_op jit(solution)/shard_map/psum | solution.py:19
  53.7 1.2 subtract_reduce_fusion
  54.9 1.2 multiply_reduce_fusion
  56.1 1.9 %multiply_convert_fusion = bf16[512,256]{1,0:T(8,128)(2,1)} fusion(f32[512,256]{1,0:T(8,128)} %param.1, f32[256]{0:T(256)S(1)} %rsqrt_multiply_fusion, f32[256]{0:T(256)S(1)} %broadcast_multiply_fusion.1, f32[512]{0:T(512)S(1)} %broadcast_multiply_fusion), kind=kLoop, calls=%fused_computation.2 | loop fusion | flops 524288 | bytes 790528 | tf_op jit(solution)/shard_map/convert_element_type | solution.py:26
  58.0 0.0 all-gather.2.cloned.1.call-update
  58.0 85.7 %all-gather.2.cloned.1.call-done = bf16[512,8192]{1,0:T(8,128)(2,1)} async-done(((bf16[512,256]{1,0:T(8,128)(2,1)}), bf16[512,8192]{1,0:T(8,128)(2,1)}) %all-gather.2.cloned.1.call-update) | async-done | bytes 8388624 | tf_op jit(solution)/shard_map/all_gather | solution.py:27
  143.8 7.9 %fusion = bf16[256,8192]{1,0:T(8,128)(2,1)} fusion(bf16[512,256]{1,0:T(8,128)(2,1)} %multiply_convert_fusion, bf16[512,8192]{1,0:T(8,128)(2,1)} %all-gather.2.cloned.1.call-done, pred[8192]{0:T(1024)(128)(4,1)S(1)} %fusion.1), kind=kOutput, calls=%fused_computation.1 | convolution fusion | flops 2151677952 | bytes 12853248 | tf_op jit(solution)/shard_map/dot_general | solution.py:9
  (4 shorter events, 0.0 us)
Async XLA Ops:
  6.5 137.2 %all-gather.2.cloned.1.call-start = ((), (), s32[]{:S(2)}) async-start(), calls=%async_computation | async-start | bytes 8650752 | tf_op jit(solution)/shard_map/all_gather | solution.py:27
Sparse Core Ops, SparseCore 0:
  58.1 85.5 all-gather.1
